TPU v7x, 32 devices: a whole 2x2x4 slice. The times are simulated.
32 devices in a mesh: tok: 16 (over z, y, core), col: 2 (over x).
Axes of the slice: x: 2, y: 2, z: 4, core: 2. Of those that a mesh axis runs over, the one named last changes fastest.
Arguments:
- hidden: bfloat16 [4096, 8192], P('tok'), may hold values from -6 to 6
- norm_gain: float32 [8192], replicated, may hold values from 0.1 to 1.9
- token_ids: int32 [4096], P('tok'), may hold values from 0 to 128000, as said below
- owner: int32 [1], replicated, may hold values from 0 to 15
- query_store: bfloat16 [16, 8192, 4096], P('tok', None, 'col'), may hold values from -0.0625 to 0.0625
- key_store: bfloat16 [16, 8192, 512], P('tok', None, 'col'), may hold values from -0.0625 to 0.0625
Outputs:
- queries: bfloat16 [4096, 4096], P('tok', 'col')
- keys: bfloat16 [4096, 512], P('tok', 'col')
- hessian: float32 [8192, 8192], P('col', 'tok')
Inputs may be any that keep to these rules, and one draw needn't show every extreme that they name: `token_ids`: id 128000 marks the first token of a document; every other id is below it.
All inputs are finite; a program needn't handle non-finite values.
Results may differ from a plain program's by a relative error of at most 0.0049.
Values may be sent and summed in bfloat16 or wider, within the bound.
A program may use at most 256 MiB of HBM per device.

v0:
```python
import jax
import jax.numpy as jnp
from jax import lax
from jax.sharding import PartitionSpec as P

HEAD = 128
SEQ = 128


begin_token = 128000
rope_base = 500000.0


def spread(array, axis, root):
    mine = lax.axis_index(axis) == root
    return lax.psum(jnp.where(mine, array, jnp.zeros_like(array)), axis)


def positions(token_ids):
    samples = token_ids.reshape(-1, SEQ)
    index = jnp.arange(SEQ, dtype=jnp.int32)
    starts = jnp.where(samples == begin_token, index[None, :], jnp.zeros_like(samples))
    latest = lax.cummax(starts, axis=1)
    return (index[None, :] - latest).reshape(-1)


def rotate(values, place, start):
    width = values.shape[1]
    dims = (start + jnp.arange(width, dtype=jnp.int32)) % HEAD
    pair = (dims[0::2] // 2).astype(jnp.float32)
    freq = jnp.power(jnp.float32(rope_base), -2.0 * pair / HEAD)
    angle = place.astype(jnp.float32)[:, None] * freq[None, :]
    cosine = jnp.cos(angle)
    sine = jnp.sin(angle)
    even = values[:, 0::2]
    odd = values[:, 1::2]
    first = even * cosine - odd * sine
    second = even * sine + odd * cosine
    return jnp.stack([first, second], axis=-1).reshape(values.shape[0], width)


def normalize(hidden, norm_gain):
    wide = hidden.astype(jnp.float32)
    meansq = jnp.mean(wide * wide, axis=-1, keepdims=True)
    return (wide * lax.rsqrt(meansq + 1e-05) * norm_gain[None, :]).astype(jnp.bfloat16)


def transposed_product(left, right):
    return lax.dot_general(
        left, right, (((0,), (0,)), ((), ())), preferred_element_type=jnp.float32
    )


def shards(hidden, norm_gain, token_ids, owner, query_store, key_store):
    normed = normalize(hidden, norm_gain)
    place = positions(token_ids)
    column = lax.axis_index("col")
    row_width = normed.shape[1] // lax.axis_size("col")
    row_block = lax.dynamic_slice_in_dim(normed, column * row_width, row_width, 1)
    total_tokens = normed.shape[0] * lax.axis_size("tok")
    weight_q, weight_k = (
        spread(query_store[0], "tok", owner[0]),
        spread(key_store[0], "tok", owner[0]),
    )
    col_block = lax.all_to_all(normed, "tok", split_axis=1, concat_axis=0, tiled=True)
    gathered = lax.all_gather(row_block, "tok", axis=0, tiled=True)
    gram = transposed_product(gathered, col_block)
    hessian = gram * (2.0 / total_tokens)
    raw_q = jnp.dot(normed, weight_q, preferred_element_type=jnp.float32)
    raw_k = jnp.dot(normed, weight_k, preferred_element_type=jnp.float32)
    queries = rotate(raw_q, place, column * weight_q.shape[1]).astype(jnp.bfloat16)
    keys = rotate(raw_k, place, column * weight_k.shape[1]).astype(jnp.bfloat16)
    return (queries, keys, hessian)


def solution(mesh):
    placed = (P("tok", None), P(), P("tok"), P(), P("tok", None, "col"), P("tok", None, "col"))
    return jax.shard_map(
        shards,
        mesh=mesh,
        in_specs=placed,
        out_specs=(P("tok", "col"), P("tok", "col"), P("col", "tok")),
        check_vma=False,
    )
```

profile of v0, /device:TPU:0, one launch (start us, length us, event | category | flops | bytes accessed | tf_op | source)
XLA Modules:
  0.0 965.0 jit_solution(8595270427040442402)
XLA Ops:
  7.9 11.1 %select_bitcast_fusion = bf16[8192,2048]{1,0:T(8,128)(2,1)} fusion(bf16[1,8192,2048]{2,1,0:T(8,128)(2,1)} %param.10, pred[]{:T(512)S(6)} %eq.17), kind=kLoop, calls=%fused_computation | loop fusion | flops 16777216 | bytes 67108864 | tf_op jit(solution)/shard_map/jit(_where)/select_n | solution.py:16
  19.0 2.3 select_bitcast_fusion.1
  21.4 0.0 all-gather.2.cloned.1.call-start
  21.4 6.4 copy.13
  27.8 3.5 fusion
  31.3 3.5 fusion.2
  34.8 2.0 copy-done
  36.8 1.4 constant_dynamic-slice_fusion
  38.3 19.9 %all-to-all-start = ((bf16[256,16,512]{0,2,1:T(8,128)(2,1)}), bf16[256,16,512]{0,2,1:T(8,128)(2,1)}, u32[]{:S(2)}, u32[]{:S(2)}) async-start(bf16[256,16,512]{0,2,1:T(8,128)(2,1)} %bitcast.31), calls=%async_computation | async-start | bytes 8388608 | tf_op jit(solution)/shard_map/all_to_all | solution.py:65
  58.2 0.2 slice.22
  58.5 0.2 slice.19
  58.7 0.3 reduce_window_max.10
  59.1 118.6 %all-to-all-done = bf16[256,16,512]{0,2,1:T(8,128)(2,1)} async-done(((bf16[256,16,512]{0,2,1:T(8,128)(2,1)}), bf16[256,16,512]{0,2,1:T(8,128)(2,1)}, u32[]{:S(2)}, u32[]{:S(2)}) %all-to-all-start) | async-done | bytes 4194336 | tf_op jit(solution)/shard_map/all_to_all | solution.py:65
  177.6 6.5 copy.16
  184.1 571.8 %all-reduce.3.cloned.1.call-done = (bf16[8192,2048]{1,0:T(8,128)(2,1)}, bf16[8192,256]{1,0:T(8,128)(2,1)}) async-done(((bf16[8192,2048]{1,0:T(8,128)(2,1)}, bf16[8192,256]{1,0:T(8,128)(2,1)}), (bf16[8192,2048]{1,0:T(8,128)(2,1)}, bf16[8192,256]{1,0:T(8,128)(2,1)})) %all-reduce.3.cloned.1.call-update) | async-done | bytes 37748752 | tf_op jit(solution)/shard_map/psum | solution.py:16
  755.8 5.2 fusion.34
  761.1 0.1 slice.21
  761.2 0.1 slice.23
  761.3 17.6 %fusion.33 = f32[256,2048]{1,0:T(8,128)S(1)} fusion(bf16[256,8192]{0,1:T(8,128)(2,1)} %copy-done, bf16[8192,2048]{1,0:T(8,128)(2,1)} %get-tuple-element.9), kind=kOutput, calls=%fused_computation.64 | convolution fusion | flops 8589934592 | bytes 39845888 | tf_op jit(solution)/shard_map/dot_general | solution.py:69
  778.9 35.1 %slice.18 = f32[256,1024]{1,0:T(8,128)S(1)} slice(f32[256,2048]{1,0:T(8,128)S(1)} %fusion.33), slice={[0:256:1], [0:2048:2]} | slice | bytes 2097152 | tf_op jit(solution)/shard_map/slice | solution.py:35
  814.0 35.9 %slice.20 = f32[256,1024]{1,0:T(8,128)} slice(f32[256,2048]{1,0:T(8,128)S(1)} %fusion.33), slice={[0:256:1], [1:2048:2]} | slice | bytes 2097152 | tf_op jit(solution)/shard_map/slice | solution.py:36
  849.9 0.6 fusion.22
  850.5 0.1 copy.15
  850.6 0.1 convert_element_type.38
  850.7 0.8 copy.18
  851.4 6.5 fusion.12
  858.0 0.1 pad_maximum_fusion
  858.1 0.9 copy.14
  859.0 0.4 convert_element_type.36
  859.4 1.4 copy.17
  860.9 72.3 %all-gather.2.cloned.1.call-done = bf16[4096,4096]{0,1:T(8,128)(2,1)} async-done(((bf16[256,4096]{0,1:T(8,128)(2,1)}), bf16[4096,4096]{0,1:T(8,128)(2,1)}) %all-gather.2.cloned.1.call-update) | async-done | bytes 33554448 | tf_op jit(solution)/shard_map/all_gather | solution.py:66
  933.2 24.9 %convolution_multiply_fusion = f32[4096,512]{1,0:T(8,128)} fusion(bf16[4096,4096]{0,1:T(8,128)(2,1)} %all-gather.2.cloned.1.call-done, bf16[4096,512]{1,0:T(8,128)(2,1)} %bitcast.32), kind=kOutput, calls=%fused_computation.6 | convolution fusion | flops 17181966336 | bytes 46137344 | tf_op jit(solution)/shard_map/dot_general | solution.py:49
  (18 shorter events, 0.2 us)
Async XLA Ops:
  7.2 748.7 %all-reduce.3.cloned.1.call-start = ((), (), s32[]{:S(2)}) async-start(), calls=%async_computation.2 | async-start | bytes 75497472 | tf_op jit(solution)/shard_map/psum | solution.py:16
  21.4 911.8 %all-gather.2.cloned.1.call-start = ((), (), s32[]{:S(2)}) async-start(), calls=%async_computation.1 | async-start | bytes 35651584 | tf_op jit(solution)/shard_map/all_gather | solution.py:66
  21.4 9.8 %copy-start.2 = (f32[8192]{0:T(1024)S(1)}, f32[8192]{0:T(1024)}, u32[]{:S(2)}) copy-start(f32[8192]{0:T(1024)} %param.7) | copy-start | bytes 98308
  27.8 3.5 copy-start.1
  34.8 2.0 copy-start
  38.2 20.4 %copy-start.3 = (s32[256]{0:T(256)S(1)}, s32[256]{0:T(256)}, u32[]{:S(2)}) copy-start(s32[256]{0:T(256)} %param.8) | copy-start | bytes 3076
  38.3 139.3 %all-to-all-start = ((bf16[256,16,512]{0,2,1:T(8,128)(2,1)}), bf16[256,16,512]{0,2,1:T(8,128)(2,1)}, u32[]{:S(2)}, u32[]{:S(2)}) async-start(bf16[256,16,512]{0,2,1:T(8,128)(2,1)} %bitcast.31), calls=%async_computation | async-start | bytes 8388608 | tf_op jit(solution)/shard_map/all_to_all | solution.py:65
Sparse Core Ops, SparseCore 0:
  21.5 734.3 all-reduce.2
  757.4 175.8 all-gather.1
where the time goes:
time: 965 us
  waiting for transfers between devices  763 us (79%)
  local copies, waits for them, and re-layouts  91.6 us (9%)
  matrix products  47.7 us (5%)
  other arithmetic  28 us (3%)
  starting transfers between devices  20 us (2%)
  between operations  14.9 us (2%)
    psum x1, waiting for transfers between devices, spread(): return lax.psum(jnp.where(mine, array, jnp.zeros_like(array)), axis)  572 us
    all_to_all x1, waiting for transfers between devices, shards(): lax.all_to_all(normed, 'tok', split_axis=1, concat_axis=0, tiled=True)  119 us
    all_gather x1, waiting for transfers between devices, shards(): gathered = lax.all_gather(row_block, 'tok', axis=0, tiled=True)  72.3 us
    slice x2, local copies, waits for them, and re-layouts, rotate(): odd = values[:, 1::2]  36 us
    slice x2, local copies, waits for them, and re-layouts, rotate(): even = values[:, 0::2]  35.2 us
    dot_general x1, matrix products, transposed_product(): lax.dot_general(left, right, (((0,), (0,)), ((), ())), preferred_element_...  24.9 us
    all_to_all x1, starting transfers between devices, shards(): lax.all_to_all(normed, 'tok', split_axis=1, concat_axis=0, tiled=True)  19.9 us
  transfers between devices with their start and end apart: 3, of which 3 were waited for; matrix products, arithmetic and copies ran while one was open for 13% of the time, Pallas kernels for 0%

commit v1 on v0

--- a/solution.py
+++ b/solution.py
@@ -11,9 +11,15 @@
 rope_base = 500000.0
 
 
-def spread(array, axis, root):
-    mine = lax.axis_index(axis) == root
-    return lax.psum(jnp.where(mine, array, jnp.zeros_like(array)), axis)
+def scatter_weights(query, key, owner):
+    groups = lax.axis_size("tok")
+    depth, width = query.shape
+    piece = width // groups
+    mine = lax.axis_index("tok") == owner
+    query = jnp.moveaxis(query.reshape(depth, groups, piece), 1, 0)
+    key = key.reshape(groups, depth * key.shape[1] // groups // piece, piece)
+    both = jnp.concatenate([query, key], axis=1)
+    return jnp.where(mine, both, jnp.zeros_like(both))
 
 
 def positions(token_ids):
@@ -26,17 +32,21 @@
 
 def rotate(values, place, start):
     width = values.shape[1]
-    dims = (start + jnp.arange(width, dtype=jnp.int32)) % HEAD
-    pair = (dims[0::2] // 2).astype(jnp.float32)
+    period = HEAD if width % HEAD == 0 else width
+    dims = (start + jnp.arange(period, dtype=jnp.int32)) % HEAD
+    pair = (dims // 2).astype(jnp.float32)
     freq = jnp.power(jnp.float32(rope_base), -2.0 * pair / HEAD)
     angle = place.astype(jnp.float32)[:, None] * freq[None, :]
-    cosine = jnp.cos(angle)
-    sine = jnp.sin(angle)
-    even = values[:, 0::2]
-    odd = values[:, 1::2]
-    first = even * cosine - odd * sine
-    second = even * sine + odd * cosine
-    return jnp.stack([first, second], axis=-1).reshape(values.shape[0], width)
+    even = dims % 2 == 0
+    sine = jnp.where(even[None, :], -jnp.sin(angle), jnp.sin(angle))
+    cosine, sine = lax.optimization_barrier((jnp.cos(angle), sine))
+    cosine = jnp.tile(cosine, (1, width // period))
+    sine = jnp.tile(sine, (1, width // period))
+    following = jnp.concatenate([values[:, 1:], values[:, :1]], axis=1)
+    previous = jnp.concatenate([values[:, -1:], values[:, :-1]], axis=1)
+    even = jnp.arange(width, dtype=jnp.int32) % 2 == 0
+    other = jnp.where(even[None, :], following, previous)
+    return values * cosine + other * sine
 
 
 def normalize(hidden, norm_gain):
@@ -58,18 +68,27 @@
     row_width = normed.shape[1] // lax.axis_size("col")
     row_block = lax.dynamic_slice_in_dim(normed, column * row_width, row_width, 1)
     total_tokens = normed.shape[0] * lax.axis_size("tok")
-    weight_q, weight_k = (
-        spread(query_store[0], "tok", owner[0]),
-        spread(key_store[0], "tok", owner[0]),
-    )
+    groups, parts = lax.axis_size("tok"), lax.axis_size("col")
+    depth, q_width = query_store.shape[1:]
+    k_width = key_store.shape[2]
+    masked = scatter_weights(query_store[0], key_store[0], owner[0])
+    gathered = lax.all_gather(row_block, "tok", axis=0, tiled=True)
     col_block = lax.all_to_all(normed, "tok", split_axis=1, concat_axis=0, tiled=True)
-    gathered = lax.all_gather(row_block, "tok", axis=0, tiled=True)
+    masked, gathered = lax.optimization_barrier((masked, gathered))
+    owned = lax.psum_scatter(masked, "tok", scatter_dimension=0, tiled=False)
     gram = transposed_product(gathered, col_block)
     hessian = gram * (2.0 / total_tokens)
-    raw_q = jnp.dot(normed, weight_q, preferred_element_type=jnp.float32)
+    key_rows = owned[depth:].reshape(depth // groups, k_width)
+    weight_k = lax.all_gather(key_rows, "tok", axis=0, tiled=True)
+    weight_q = lax.all_to_all(owned[:depth], "col", split_axis=0, concat_axis=1, tiled=True)
+    partial = jnp.dot(gathered, weight_q, preferred_element_type=jnp.float32).astype(jnp.bfloat16)
+    partial = lax.all_to_all(partial, "col", split_axis=1, concat_axis=0, tiled=True)
+    partial = partial.reshape(parts, total_tokens, q_width // groups).astype(jnp.float32)
+    summed = jnp.sum(partial, axis=0).astype(jnp.bfloat16)
+    raw_q = lax.all_to_all(summed, "tok", split_axis=0, concat_axis=1, tiled=True).astype(jnp.float32)
     raw_k = jnp.dot(normed, weight_k, preferred_element_type=jnp.float32)
-    queries = rotate(raw_q, place, column * weight_q.shape[1]).astype(jnp.bfloat16)
-    keys = rotate(raw_k, place, column * weight_k.shape[1]).astype(jnp.bfloat16)
+    queries = rotate(raw_q, place, column * q_width).astype(jnp.bfloat16)
+    keys = rotate(raw_k, place, column * k_width).astype(jnp.bfloat16)
     return (queries, keys, hessian)
 
 

time: 965 us -> 807 us (0.84)
  waiting for transfers between devices: 763 us -> 564 us
  blocking collectives: 0 us -> 28.7 us
  other arithmetic: 28 us -> 39.7 us
    psum x1 -> x0, waiting for transfers between devices: 572 us -> none  [spread(): return lax.psum(jnp.where(mine, array, jnp.zeros_like(array)), axis)]
    reduce_scatter x0 -> x1, waiting for transfers between devices: none -> 367 us  [shards(): owned = lax.psum_scatter(masked, 'tok', scatter_dimension=0, tiled=False)]
    slice x6 -> x10, local copies, waits for them, and re-layouts: 71.6 us -> 4.55 us  [the longest x3 4.01 us: shards(): owned[:depth]]
    unnamed x11 -> x10, local copies, waits for them, and re-layouts: 10.6 us -> 49.7 us
    all_to_all x1, waiting for transfers between devices: 119 us -> 82 us  [shards(): lax.all_to_all(normed, 'tok', split_axis=1, concat_axis=0, tiled=True)]
    all_to_all x0 -> x1, blocking collectives: none -> 28.7 us  [shards(): lax.all_to_all(owned[:depth], 'col', split_axis=0, concat_axis=1, tiled=T...]
    all_gather x1, waiting for transfers between devices: 72.3 us -> 97.2 us  [shards(): gathered = lax.all_gather(row_block, 'tok', axis=0, tiled=True)]
    all_to_all x0 -> x2, starting transfers between devices: none -> 22.9 us  [the longest x1 19.1 us: shards(): lax.all_to_all(summed, 'tok', split_axis=0, concat_axis=1, tiled=True)]
  transfers between devices with their start and end apart: 3 -> 6, of which waited for: 3 -> 4; matrix products, arithmetic and copies ran while one was open for 13% -> 18% of each run, Pallas kernels for 0% -> 0%
where the time goes in v1:
time: 807 us; the launch traced here: 805 us
  waiting for transfers between devices  564 us (70%)
  local copies, waits for them, and re-layouts  83.9 us (10%)
  matrix products  47 us (6%)
  other arithmetic  39.7 us (5%)
  blocking collectives  28.7 us (4%)
  starting transfers between devices  27.7 us (3%)
  between operations  14.6 us (2%)
    reduce_scatter x1, waiting for transfers between devices, shards(): owned = lax.psum_scatter(masked, 'tok', scatter_dimension=0, tiled=False)  367 us
    all_gather x1, waiting for transfers between devices, shards(): gathered = lax.all_gather(row_block, 'tok', axis=0, tiled=True)  97.2 us
    all_to_all x1, waiting for transfers between devices, shards(): lax.all_to_all(normed, 'tok', split_axis=1, concat_axis=0, tiled=True)  82 us
    unnamed x10, local copies, waits for them, and re-layouts  49.7 us
    all_to_all x1, blocking collectives, shards(): lax.all_to_all(owned[:depth], 'col', split_axis=0, concat_axis=1, tiled=T...  28.7 us
    select_n x1, other arithmetic, scatter_weights(): return jnp.where(mine, both, jnp.zeros_like(both))  26.2 us
    dot_general x1, matrix products, transposed_product(): lax.dot_general(left, right, (((0,), (0,)), ((), ())), preferred_element_...  24.9 us
    all_to_all x1, starting transfers between devices, shards(): lax.all_to_all(summed, 'tok', split_axis=0, concat_axis=1, tiled=True)  19.1 us
  transfers between devices with their start and end apart: 6, of which 4 were waited for; matrix products, arithmetic and copies ran while one was open for 18% of the time, Pallas kernels for 0%

profile of v1, /device:TPU:0, one launch (start us, length us, event | category | flops | bytes accessed | tf_op | source)
XLA Modules:
  0.0 805.3 jit_solution(15979491597854379101)
XLA Ops:
  7.2 6.4 copy.38
  13.6 3.3 fusion
  16.9 4.3 fusion.2
  21.2 3.1 constant_dynamic-slice_fusion
  24.4 7.1 reshape_squeeze.7
  31.4 6.3 copy.37
  37.8 41.1 %copy.36 = bf16[1,8192,2048]{1,2,0:T(8,128)(2,1)} copy(bf16[1,8192,2048]{2,1,0:T(8,128)(2,1)} %param.10) | data formatting | bytes 67108864 | tf_op args[4]
  79.6 26.2 %maximum_select_fusion = bf16[16,9216,128]{1,2,0:T(8,128)(2,1)} fusion(bf16[16,1024,128]{1,2,0:T(8,128)(2,1)} %copy.37, bf16[16,8192,128]{1,2,0:T(8,128)(2,1)} %bitcast.39, pred[]{:T(512)S(6)} %eq.51), kind=kLoop, calls=%fused_computation | loop fusion | flops 94371840 | bytes 75497472 | tf_op jit(solution)/shard_map/jit(_where)/select_n | solution.py:22
  105.8 97.2 %all-gather.3.cloned.1.call-done = bf16[4096,4096]{0,1:T(8,128)(2,1)} async-done(((bf16[256,4096]{0,1:T(8,128)(2,1)}), bf16[4096,4096]{0,1:T(8,128)(2,1)}) %all-gather.3.cloned.1.call-update) | async-done | bytes 33554448 | tf_op jit(solution)/shard_map/all_gather | solution.py:75
  203.0 366.7 %reduce-scatter.2.cloned.1.call-done = bf16[1,9216,128]{1,2,0:T(8,128)(2,1)} async-done(((bf16[16,9216,128]{1,2,0:T(8,128)(2,1)}), bf16[1,9216,128]{1,2,0:T(8,128)(2,1)}) %reduce-scatter.2.cloned.1.call-update) | async-done | bytes 2359312 | tf_op jit(solution)/shard_map/reduce_scatter | solution.py:78
  569.7 1.6 slice-done
  571.3 2.4 copy.39
  573.7 28.7 %all_to_all.64 = bf16[2,4096,128]{2,1,0:T(8,128)(2,1)S(1)} all-to-all(bf16[2,4096,128]{2,1,0:T(8,128)(2,1)} %bitcast.44), channel_id=1, replica_groups=mesh['tok'=16,'col'=2] {'col'}, dimensions={0} | all-to-all | bytes 4194304 | tf_op jit(solution)/shard_map/all_to_all | solution.py:83
  602.4 4.7 all-to-all-start.3
  607.4 0.8 reshape.186
  608.2 2.7 copy.40
  610.9 16.9 %convolution_convert_fusion = bf16[4096,256]{0,1:T(8,128)(2,1)} fusion(bf16[4096,256]{0,1:T(8,128)(2,1)} %bitcast.47, bf16[4096,4096]{0,1:T(8,128)(2,1)} %all-gather.3.cloned.1.call-done), kind=kOutput, calls=%fused_computation.7 | convolution fusion | flops 8590983168 | bytes 37748736 | tf_op jit(solution)/shard_map/dot_general | solution.py:84
  627.8 82.0 %all-to-all-done.3 = bf16[256,16,512]{0,2,1:T(8,128)(2,1)} async-done(((bf16[256,16,512]{0,2,1:T(8,128)(2,1)}), bf16[256,16,512]{0,2,1:T(8,128)(2,1)}, u32[]{:S(2)}, u32[]{:S(2)}) %all-to-all-start.3) | async-done | bytes 4194336 | tf_op jit(solution)/shard_map/all_to_all | solution.py:76
  709.8 3.8 all-to-all-start.1
  714.0 1.8 negate_select_fusion
  715.8 6.3 copy.44
  722.1 17.7 %all-to-all-done.1 = bf16[4096,2,128]{0,2,1:T(8,128)(2,1)S(1)} async-done(((bf16[4096,2,128]{0,2,1:T(8,128)(2,1)}), bf16[4096,2,128]{0,2,1:T(8,128)(2,1)S(1)}, u32[]{:S(2)}, u32[]{:S(2)}) %all-to-all-start.1) | async-done | bytes 2097184 | tf_op jit(solution)/shard_map/all_to_all | solution.py:85
  739.8 0.7 reduce_sum.22
  740.5 1.3 copy.41
  741.8 19.1 %all-to-all-start.2 = ((bf16[16,256,128]{2,1,0:T(8,128)(2,1)}), bf16[16,256,128]{2,1,0:T(8,128)(2,1)S(1)}, u32[]{:S(2)}, u32[]{:S(2)}) async-start(bf16[16,256,128]{2,1,0:T(8,128)(2,1)} %bitcast.7), calls=%async_computation.3 | async-start | bytes 2097152 | tf_op jit(solution)/shard_map/all_to_all | solution.py:88
  760.9 24.9 %convolution_multiply_fusion = f32[4096,512]{1,0:T(8,128)} fusion(bf16[4096,4096]{0,1:T(8,128)(2,1)} %all-gather.3.cloned.1.call-done, bf16[4096,512]{1,0:T(8,128)(2,1)} %bitcast.45), kind=kOutput, calls=%fused_computation.6 | convolution fusion | flops 17181966336 | bytes 46137344 | tf_op jit(solution)/shard_map/dot_general | solution.py:59
  785.9 1.6 convert_bitcast_fusion
  787.4 1.9 copy.42
  789.7 1.5 fusion.5
  791.2 1.4 copy.45
  792.6 5.2 fusion.22
  798.1 0.8 copy.46
  (31 shorter events, 1.2 us)
Async XLA Ops:
  7.2 195.8 %all-gather.3.cloned.1.call-start = ((), (), s32[]{:S(2)}) async-start(), calls=%async_computation.5 | async-start | bytes 35651584 | tf_op jit(solution)/shard_map/all_gather | solution.py:75
  13.6 3.3 copy-start.1
  24.3 545.4 %reduce-scatter.2.cloned.1.call-start = ((), (), s32[]{:S(2)}) async-start(), calls=%async_computation.6 | async-start | bytes 40108032 | tf_op jit(solution)/shard_map/reduce_scatter | solution.py:78
  569.7 1.6 slice-start
  602.4 4.8 slice-start.1
  602.4 107.4 %all-to-all-start.3 = ((bf16[256,16,512]{0,2,1:T(8,128)(2,1)}), bf16[256,16,512]{0,2,1:T(8,128)(2,1)}, u32[]{:S(2)}, u32[]{:S(2)}) async-start(bf16[256,16,512]{0,2,1:T(8,128)(2,1)} %bitcast.42), calls=%async_computation.4 | async-start | bytes 8388608 | tf_op jit(solution)/shard_map/all_to_all | solution.py:76
  607.1 185.5 %all-gather.5.cloned.1.call-start = ((), (), s32[]{:S(2)}) async-start(), calls=%async_computation.7 | async-start | bytes 4456448 | tf_op jit(solution)/shard_map/all_gather | solution.py:82
  627.8 85.8 %copy-start.2 = (s32[256]{0:T(256)S(1)}, s32[256]{0:T(256)}, u32[]{:S(2)}) copy-start(s32[256]{0:T(256)} %param.8) | copy-start | bytes 3076
  709.8 30.0 %all-to-all-start.1 = ((bf16[4096,2,128]{0,2,1:T(8,128)(2,1)}), bf16[4096,2,128]{0,2,1:T(8,128)(2,1)S(1)}, u32[]{:S(2)}, u32[]{:S(2)}) async-start(bf16[4096,2,128]{0,2,1:T(8,128)(2,1)} %bitcast.46), calls=%async_computation.2 | async-start | bytes 4194304 | tf_op jit(solution)/shard_map/all_to_all | solution.py:85
  741.8 44.1 %all-to-all-start.2 = ((bf16[16,256,128]{2,1,0:T(8,128)(2,1)}), bf16[16,256,128]{2,1,0:T(8,128)(2,1)S(1)}, u32[]{:S(2)}, u32[]{:S(2)}) async-start(bf16[16,256,128]{2,1,0:T(8,128)(2,1)} %bitcast.7), calls=%async_computation.3 | async-start | bytes 2097152 | tf_op jit(solution)/shard_map/all_to_all | solution.py:88
  792.6 5.3 copy-start
Sparse Core Ops, SparseCore 0:
  24.4 178.4 all-gather.2
  207.2 362.4 reduce-scatter.1
  610.1 93.2 all-gather.4
